TPU v7x, 256 devices: a whole 4x4x8 slice. The times are simulated.
256 devices in a mesh: chain: 16 (over z, core), dp: 16 (over y, x).
Axes of the slice: x: 4, y: 4, z: 8, core: 2. Of those that a mesh axis runs over, the one named last changes fastest.
Arguments:
- images_in: float32 [16, 1024, 1024], P('chain', 'dp'), may hold values from -8 to 8
- images_mid: float32 [16, 1024, 1024], P('chain', 'dp'), may hold values from -8 to 8
- images_out: float32 [16, 1024, 1000], P('chain', 'dp'), may hold values from -8 to 8
- ends_in: float32 [2, 1024, 1024], P(None, 'dp'), may hold values from -8 to 8
- ends_mid: float32 [2, 1024, 1024], P(None, 'dp'), may hold values from -8 to 8
- ends_out: float32 [2, 1024, 1000], P(None, 'dp'), may hold values from -8 to 8
- data_pool: bfloat16 [28672, 1024], P('dp'), may hold values from -6 to 6
- batch_rows: int32 [16, 14336], P('chain', 'dp'), may hold values from 0 to 1791
- labels: int32 [16, 14336], P('chain', 'dp'), may hold values from 0 to 999
- climbing: int32 [16], P('chain'), may hold values 0 or 1
Outputs:
- new_in: float32 [16, 1024, 1024], P('chain', 'dp')
- new_mid: float32 [16, 1024, 1024], P('chain', 'dp')
- new_out: float32 [16, 1024, 1000], P('chain', 'dp')
- energies: float32 [16], P('chain')
- arc_share: float32 [16], P('chain')
- bend: float32 [16], P('chain')
Inputs may be any that keep to these rules, and one draw needn't show every extreme that they name: batch_rows[i, b] names a row of the pool shard held by dp index b // 896.
All inputs are finite; a program needn't handle non-finite values. No bound on the sum of `climbing` on one device may be relied on, other than what follows from the above.
Results may differ from a plain program's by a relative error of at most 0.0023.
Values may be sent and summed in bfloat16 or wider, within the bound.
A program may use at most 128 MiB of HBM per device.

v0:
```python
import jax
import jax.numpy as jnp
from jax import lax
from jax.sharding import Mesh
from jax.sharding import PartitionSpec as P

DP = ("dp_0", "dp_1")
SPRING = 0.03
EPS = 1e-06


def for_sending(value):

    def short(part):
        return part.astype(jnp.bfloat16) if part.dtype == jnp.float32 else part

    return jax.tree.map(short, value)


def gather_axes(value, axes, dim):
    if not axes:
        return value
    nearer = lax.all_gather(value, axes[-1], axis=dim, tiled=True)
    return gather_axes(nearer, axes[:-1], dim)


def in_one_piece(arrays, axis, dim, along):
    both = jnp.concatenate(arrays, axis=along)
    whole, at, gathered = (lax.psum_scatter(both, axis, scatter_dimension=dim, tiled=True), 0, [])
    for a in arrays:
        gathered.append(lax.slice_in_dim(whole, at, at + a.shape[along], axis=along))
        at += a.shape[along]
    return tuple(gathered)


def passed_along(block, axis, distance):
    devices = range(lax.axis_size(axis))
    route = [(i - distance, i) for i in devices if i - distance in devices]
    return lax.ppermute(block, axis, route)


def over_axes(value, axes):
    for axis in axes:
        value = lax.psum(value, axis)
    return value


def joined_along(blocks, dim):
    blocks = jnp.moveaxis(blocks, 0, dim)
    dims = blocks.shape
    return blocks.reshape(*dims[:dim], dims[dim] * dims[dim + 1], *dims[dim + 2 :])


def copy_for_each(value, axis):
    peers = lax.axis_size(axis)
    return lax.all_to_all(
        jnp.broadcast_to(value[None], (peers, *value.shape)), axis, 0, 0, tiled=True
    )


def gathered_copies(value, axis, dim):
    return joined_along(copy_for_each(value, axis), dim)


def silu_slope(pre):
    sig = jax.nn.sigmoid(pre)
    return sig * (1.0 + pre * (1.0 - sig))


def dot_nt(left, right):
    return lax.dot_general(
        left, right, (((1,), (1,)), ((), ())), preferred_element_type=jnp.float32
    )


def dot_tn(left, right):
    return lax.dot_general(
        left, right, (((0,), (0,)), ((), ())), preferred_element_type=jnp.float32
    )


def inner(first, second):
    total = jnp.float32(0.0)
    for left, right in zip(first, second):
        total = total + jnp.sum(left * right)
    return total


def on_device(
    images_in,
    images_mid,
    images_out,
    ends_in,
    ends_mid,
    ends_out,
    data_pool,
    batch_rows,
    labels,
    climbing,
):
    own = (images_in[0], images_mid[0], images_out[0])
    width = data_pool.shape[1]
    hidden_units = images_in.shape[2]
    classes = images_out.shape[2]
    groups = lax.axis_size(DP)
    factors = (width ** (-0.5), hidden_units ** (-0.5), width ** (-0.5))
    lowered = tuple(((p * f).astype(jnp.bfloat16) for p, f in zip(own, factors)))
    w_in, w_mid, w_out = jax.tree.map(
        lambda part, own: part.astype(own.dtype),
        jax.tree.map(lambda part: gather_axes(part, DP, 0), for_sending(lowered)),
        lowered,
    )
    rows = data_pool[batch_rows[0]]
    batch = rows.shape[0] * groups
    pre = jnp.dot(rows, w_in, preferred_element_type=jnp.float32)
    hid = jax.nn.silu(pre).astype(jnp.bfloat16)
    resid = (
        rows.astype(jnp.float32) + jnp.dot(hid, w_mid, preferred_element_type=jnp.float32)
    ).astype(jnp.bfloat16)
    logits = jnp.dot(resid, w_out, preferred_element_type=jnp.float32)
    target = (labels[0][:, None] == jnp.arange(classes, dtype=jnp.int32)[None, :]).astype(
        jnp.float32
    )
    err = logits - target
    norm = 1.0 / (batch * classes)
    energy_part = 0.5 * norm * jnp.sum(err * err)
    d_logits = (err * norm).astype(jnp.bfloat16)
    d_resid = dot_nt(d_logits, w_out).astype(jnp.bfloat16)
    d_pre = (dot_nt(d_resid, w_mid) * silu_slope(pre)).astype(jnp.bfloat16)
    summed = tuple(
        (
            part.astype(jnp.float32)
            for part in in_one_piece(
                (
                    dot_tn(rows, d_pre).astype(jnp.bfloat16),
                    dot_tn(hid, d_resid).astype(jnp.bfloat16),
                    dot_tn(resid, d_logits).astype(jnp.bfloat16),
                ),
                DP,
                0,
                1,
            )
        )
    )
    grads = tuple((g * f for g, f in zip(summed, factors)))
    index = lax.axis_index("chain")
    count = lax.axis_size("chain")
    ends = (ends_in, ends_mid, ends_out)
    left = (
        passed_along(own[0].astype(jnp.bfloat16), "chain", 1).astype(jnp.float32),
        passed_along(own[1].astype(jnp.bfloat16), "chain", 1).astype(jnp.float32),
        passed_along(own[2].astype(jnp.bfloat16), "chain", 1).astype(jnp.float32),
    )
    right = (
        passed_along(own[0].astype(jnp.bfloat16), "chain", -1).astype(jnp.float32),
        passed_along(own[1].astype(jnp.bfloat16), "chain", -1).astype(jnp.float32),
        passed_along(own[2].astype(jnp.bfloat16), "chain", -1).astype(jnp.float32),
    )
    left = tuple((jnp.where(index == 0, e[0], piece) for e, piece in zip(ends, left)))
    right = tuple((jnp.where(index == count - 1, e[1], piece) for e, piece in zip(ends, right)))
    ahead = tuple((r - o for r, o in zip(right, own)))
    behind = tuple((o - l for o, l in zip(own, left)))
    sq_ahead, sq_behind, cross, g_ahead, g_behind, g_g, energy = (
        over_axes(inner(ahead, ahead), DP),
        over_axes(inner(behind, behind), DP),
        over_axes(inner(ahead, behind), DP),
        over_axes(inner(grads, ahead), DP),
        over_axes(inner(grads, behind), DP),
        over_axes(inner(grads, grads), DP),
        over_axes(energy_part, DP),
    )
    len_ahead = jnp.sqrt(sq_ahead + EPS)
    len_behind = jnp.sqrt(sq_behind + EPS)
    raw_sq = (
        sq_ahead / (len_ahead * len_ahead)
        + sq_behind / (len_behind * len_behind)
        + 2.0 * cross / (len_ahead * len_behind)
    )
    raw_len = jnp.sqrt(raw_sq + EPS)
    tau = tuple(((a / len_ahead + b / len_behind) / raw_len for a, b in zip(ahead, behind)))
    along = (g_ahead / len_ahead + g_behind / len_behind) / raw_len
    tau_sq = raw_sq / (raw_sq + EPS)
    pair = jnp.stack([len_behind, len_ahead])[None, :]
    table = gathered_copies(pair, "chain", 0)
    order = jnp.arange(table.shape[0], dtype=jnp.int32)
    arc = jnp.sum(jnp.where(order <= index, table[:, 0], 0.0))
    band = jnp.sum(table[:, 0]) + table[-1, 1]
    goal = (index + 1).astype(jnp.float32) / (count + 1) * band
    coef = jnp.where(climbing[0] == 1, 2.0 * along, along + SPRING * (goal - arc) / band)
    force = tuple((-g + coef * t for g, t in zip(grads, tau)))
    force_sq = g_g - 2.0 * coef * along + coef * coef * tau_sq
    scale = band / (count + 1) / jnp.sqrt(force_sq + EPS)
    new = tuple(((o + scale * f)[None] for o, f in zip(own, force)))
    return (new[0], new[1], new[2], energy[None], (arc / band)[None], (0.5 * raw_len)[None])


def solution(mesh):
    torus = Mesh(mesh.devices.reshape(mesh.shape["chain"], 4, 4), ("chain", "dp_0", "dp_1"))
    in_specs = (
        P("chain", DP, None),
        P("chain", DP, None),
        P("chain", DP, None),
        P(None, DP, None),
        P(None, DP, None),
        P(None, DP, None),
        P(DP, None),
        P("chain", DP),
        P("chain", DP),
        P("chain"),
    )
    out_specs = (
        P("chain", DP, None),
        P("chain", DP, None),
        P("chain", DP, None),
        P("chain"),
        P("chain"),
        P("chain"),
    )
    return jax.shard_map(
        on_device, mesh=torus, in_specs=in_specs, out_specs=out_specs, check_vma=False
    )
```

profile of v0, /device:TPU:1, one launch (start us, length us, event | category | flops | bytes accessed | tf_op | source)
XLA Modules:
  0.0 326.4 jit_solution(15012936727917754198)
XLA Ops:
  8.2 12.8 %all_gather.18 = bf16[256,1024]{1,0:T(8,128)(2,1)} all-gather(bf16[64,1024]{1,0:T(8,128)(2,1)S(1)} %fusion.10), channel_id=1, replica_groups=mesh['chain'=16,'dp_0'=4,'dp_1'=4] {'dp_1'}, dimensions={0}, use_global_device_ids=true | all-gather | bytes 655360 | tf_op jit(solution)/shard_map/all_gather | solution.py:23
  22.0 10.7 %all_gather.20 = bf16[256,1024]{1,0:T(8,128)(2,1)} all-gather(bf16[64,1024]{1,0:T(8,128)(2,1)S(1)} %fusion.7), channel_id=1, replica_groups=mesh['chain'=16,'dp_0'=4,'dp_1'=4] {'dp_1'}, dimensions={0}, use_global_device_ids=true | all-gather | bytes 655360 | tf_op jit(solution)/shard_map/all_gather | solution.py:23
  33.8 11.5 %all_gather.22 = bf16[256,1000]{1,0:T(8,128)(2,1)} all-gather(bf16[64,1000]{1,0:T(8,128)(2,1)S(1)} %fusion.4), channel_id=1, replica_groups=mesh['chain'=16,'dp_0'=4,'dp_1'=4] {'dp_1'}, dimensions={0}, use_global_device_ids=true | all-gather | bytes 640000 | tf_op jit(solution)/shard_map/all_gather | solution.py:23
  45.4 7.7 %gather_fusion = bf16[896,1024]{1,0:T(8,128)(2,1)S(1)} fusion(bf16[1792,1024]{1,0:T(8,128)(2,1)} %param.16, s32[1024]{0:T(1024)S(1)} %pad_clamp_fusion), kind=kCustom, calls=%fused_computation | custom fusion | bytes 3673600 | tf_op jit(solution)/shard_map/gather | solution.py:113
  53.1 6.2 %all-gather.4.cloned.1.call-done = bf16[1024,1024]{1,0:T(8,128)(2,1)} async-done(((bf16[256,1024]{1,0:T(8,128)(2,1)}), bf16[1024,1024]{1,0:T(8,128)(2,1)}) %all-gather.4.cloned.1.call-update) | async-done | bytes 2097168 | tf_op jit(solution)/shard_map/all_gather | solution.py:23
  59.3 5.4 %fusion.23 = f32[896,1024]{1,0:T(8,128)} fusion(bf16[896,1024]{1,0:T(8,128)(2,1)S(1)} %gather_fusion, bf16[1024,1024]{1,0:T(8,128)(2,1)} %all-gather.4.cloned.1.call-done), kind=kOutput, calls=%fused_computation.72 | convolution fusion | flops 1879048192 | bytes 7602176 | tf_op jit(solution)/shard_map/dot_general | solution.py:115
  64.7 29.8 %all-gather.6.cloned.1.call-done = bf16[1024,1024]{1,0:T(8,128)(2,1)} async-done(((bf16[256,1024]{1,0:T(8,128)(2,1)}), bf16[1024,1024]{1,0:T(8,128)(2,1)}) %all-gather.6.cloned.1.call-update) | async-done | bytes 2097168 | tf_op jit(solution)/shard_map/all_gather | solution.py:23
  94.5 6.2 %add_convert_fusion = bf16[896,1024]{1,0:T(8,128)(2,1)} fusion(bf16[896,1024]{1,0:T(8,128)(2,1)S(1)} %gather_fusion, bf16[1024,1024]{1,0:T(8,128)(2,1)} %all-gather.6.cloned.1.call-done, f32[896,1024]{1,0:T(8,128)} %fusion.23), kind=kOutput, calls=%fused_computation.3 | convolution fusion | flops 1886388224 | bytes 9437184 | tf_op jit(solution)/shard_map/dot_general | solution.py:118
  100.7 29.1 %all-gather.8.cloned.1.call-done = bf16[1024,1000]{1,0:T(8,128)(2,1)} async-done(((bf16[256,1000]{1,0:T(8,128)(2,1)}), bf16[1024,1000]{1,0:T(8,128)(2,1)}) %all-gather.8.cloned.1.call-update) | async-done | bytes 2048016 | tf_op jit(solution)/shard_map/all_gather | solution.py:23
  129.7 5.6 %multiply_reduce_fusion = (f32[]{:T(128)}, f32[896,1000]{0,1:T(8,128)S(1)}) fusion(s32[896]{0:T(1024)S(1)} %reduce.2, bf16[896,1024]{1,0:T(8,128)(2,1)} %add_convert_fusion, bf16[1024,1000]{1,0:T(8,128)(2,1)} %all-gather.8.cloned.1.call-done), kind=kOutput, calls=%fused_computation.6 | convolution fusion | flops 1839488000 | bytes 7470596 | tf_op jit(solution)/shard_map/dot_general | solution.py:120
  135.3 3.6 %convolution_convert_fusion.2 = bf16[1024,1000]{0,1:T(8,128)(2,1)} fusion(bf16[896,1024]{1,0:T(8,128)(2,1)S(1)} %copy-done.13, f32[896,1000]{0,1:T(8,128)S(1)} %get-tuple-element.59, s32[896]{0:T(1024)S(1)} %reduce.2), kind=kOutput, calls=%fused_computation.12 | convolution fusion | flops 1840512000 | bytes 7470592 | tf_op jit(solution)/shard_map/dot_general | solution.py:77
  142.4 2.7 convolution_convert_fusion
  145.1 9.9 %convolution_convert_fusion.1 = bf16[1024,1024]{0,1:T(8,128)(2,1)} fusion(bf16[896,1024]{1,0:T(8,128)(2,1)} %copy-done.3, f32[896,1024]{1,0:T(8,128)} %fusion.23, bf16[896,1024]{1,0:T(8,128)(2,1)} %copy-done.14, bf16[1024,1024]{1,0:T(8,128)(2,1)} %all-gather.6.cloned.1.call-done), kind=kOutput, calls=%fused_computation.11 | convolution fusion | flops 3767402496 | bytes 11534336 | tf_op jit(solution)/shard_map/dot_general | solution.py:77
  155.0 5.5 %pad_maximum_fusion = bf16[1024,3048]{0,1:T(8,128)(2,1)} fusion(bf16[1024,1000]{0,1:T(8,128)(2,1)} %convolution_convert_fusion.2, bf16[1024,1024]{0,1:T(8,128)(2,1)S(1)} %convolution_convert_fusion, bf16[1024,1024]{0,1:T(8,128)(2,1)} %convolution_convert_fusion.1), kind=kLoop, calls=%fused_computation.1 | loop fusion | flops 18726912 | bytes 12484608 | tf_op jit(solution)/shard_map/concatenate | solution.py:28
  160.5 8.8 %copy.44 = bf16[1024,3048]{1,0:T(8,128)(2,1)} copy(bf16[1024,3048]{0,1:T(8,128)(2,1)} %pad_maximum_fusion) | data formatting | bytes 12484608
  170.3 4.0 %collective-permute-start = (bf16[64,1024]{1,0:T(8,128)(2,1)S(1)}, bf16[64,1024]{1,0:T(8,128)(2,1)S(1)}, u32[]{:S(2)}, u32[]{:S(2)}) collective-permute-start(bf16[64,1024]{1,0:T(8,128)(2,1)S(1)} %bitcast_convert_fusion.2), channel_id=1, source_target_pairs={{0,16},{16,32},{32,48},{48,64},{64,80},{80,96},{96,112},{112,128},... | collective-permute-start | bytes 393224 | tf_op jit(solution)/shard_map/ppermute | solution.py:39
  176.3 3.6 %collective-permute-start.1 = (bf16[64,1024]{1,0:T(8,128)(2,1)S(1)}, bf16[64,1024]{1,0:T(8,128)(2,1)S(1)}, u32[]{:S(2)}, u32[]{:S(2)}) collective-permute-start(bf16[64,1024]{1,0:T(8,128)(2,1)S(1)} %bitcast_convert_fusion.1), channel_id=1, source_target_pairs={{0,16},{16,32},{32,48},{48,64},{64,80},{80,96},{96,112},{112,128},... | collective-permute-start | bytes 393224 | tf_op jit(solution)/shard_map/ppermute | solution.py:39
  182.5 3.6 %collective-permute-start.2 = (bf16[64,1000]{1,0:T(8,128)(2,1)}, bf16[64,1000]{1,0:T(8,128)(2,1)}, u32[]{:S(2)}, u32[]{:S(2)}) collective-permute-start(bf16[64,1000]{1,0:T(8,128)(2,1)} %bitcast_convert_fusion), channel_id=1, source_target_pairs={{0,16},{16,32},{32,48},{48,64},{64,80},{80,96},{96,112},{112,128},... | collective-permute-start | bytes 384008 | tf_op jit(solution)/shard_map/ppermute | solution.py:39
  190.7 63.8 %reduce-scatter.4.cloned.1.call-done = bf16[64,3048]{1,0:T(8,128)(2,1)} async-done(((bf16[1024,3048]{1,0:T(8,128)(2,1)}), bf16[64,3048]{1,0:T(8,128)(2,1)}) %reduce-scatter.4.cloned.1.call-update) | async-done | bytes 390160 | tf_op jit(solution)/shard_map/reduce_scatter | solution.py:29
  254.5 2.4 multiply_reduce_fusion.11
  270.2 8.7 %all-reduce.1 = (f32[]{:T(128)}, f32[]{:T(128)}, f32[]{:T(128)}, f32[]{:T(128)}, f32[]{:T(128)}, /*index=5*/f32[]{:T(128)}, f32[]{:T(128)}) all-reduce(f32[]{:T(128)S(6)} %add.155, f32[]{:T(128)S(6)} %add.152, f32[]{:T(128)S(6)} %add.172, f32[]{:T(128)S(6)} %add.166, ...), channel_id=1, replica_groups=mesh['chain'=16,'dp_0'=4,'dp_1'=4] {'dp_0'}, use_global_device_ids=true, to_apply=%region_8.9 | all-reduce | flops 7 | bytes 56 | tf_op jit(solution)/shard_map/psum | solution.py:44
  279.0 7.3 %all-reduce = (f32[]{:T(128)}, f32[]{:T(128)}, f32[]{:T(128)}, f32[]{:T(128)}, f32[]{:T(128)}, /*index=5*/f32[]{:T(128)}, f32[1]{0:T(128)}) all-reduce(f32[]{:T(128)} %get-tuple-element.43, f32[]{:T(128)} %get-tuple-element.44, f32[]{:T(128)} %get-tuple-element.45, ...), channel_id=1, replica_groups=mesh['chain'=16,'dp_0'=4,'dp_1'=4] {'dp_1'}, use_global_device_ids=true, to_apply=%region_9.10 | all-reduce | flops 7 | bytes 56 | tf_op jit(solution)/shard_map/psum | solution.py:44
  290.4 13.3 %all-to-all-start = ((f32[16,1,2]{2,1,0:T(1,128)}), f32[16,1,2]{2,1,0:T(1,128)S(1)}, u32[]{:S(2)}, u32[]{:S(2)}) async-start(f32[16,1,2]{2,1,0:T(1,128)} %broadcast_in_dim.29), calls=%async_computation | async-start | bytes 16384 | tf_op jit(solution)/shard_map/all_to_all | solution.py:56
  305.1 5.6 %all-to-all-done = f32[16,1,2]{2,1,0:T(1,128)S(1)} async-done(((f32[16,1,2]{2,1,0:T(1,128)}), f32[16,1,2]{2,1,0:T(1,128)S(1)}, u32[]{:S(2)}, u32[]{:S(2)}) %all-to-all-start) | async-done | bytes 160 | tf_op jit(solution)/shard_map/all_to_all | solution.py:56
  (66 shorter events, 21.5 us)
Async XLA Ops:
  7.2 38.1 %copy-start.9 = (s32[1,896]{1,0:T(1,128)S(1)}, s32[1,896]{1,0:T(1,128)}, u32[]{:S(2)}) copy-start(s32[1,896]{1,0:T(1,128)} %param.17) | copy-start | bytes 10756
  7.2 52.1 %all-gather.4.cloned.1.call-start = ((), (), s32[]{:S(2)}) async-start(), calls=%async_computation.2 | async-start | bytes 2621440 | tf_op jit(solution)/shard_map/all_gather | solution.py:23
  21.0 73.5 %all-gather.6.cloned.1.call-start = ((), (), s32[]{:S(2)}) async-start(), calls=%async_computation.3 | async-start | bytes 2621440 | tf_op jit(solution)/shard_map/all_gather | solution.py:23
  32.7 97.0 %all-gather.8.cloned.1.call-start = ((), (), s32[]{:S(2)}) async-start(), calls=%async_computation.4 | async-start | bytes 2621440 | tf_op jit(solution)/shard_map/all_gather | solution.py:23
  45.2 209.3 %reduce-scatter.4.cloned.1.call-start = ((), (), s32[]{:S(2)}) async-start(), calls=%async_computation.5 | async-start | bytes 6684672 | tf_op jit(solution)/shard_map/reduce_scatter | solution.py:29
  45.3 7.8 %copy-start.10 = (s32[1,896]{1,0:T(1,128)S(1)}, s32[1,896]{1,0:T(1,128)}, u32[]{:S(2)}) copy-start(s32[1,896]{1,0:T(1,128)} %param.18) | copy-start | bytes 10756
  53.1 41.4 %copy-start.3 = (bf16[896,1024]{1,0:T(8,128)(2,1)}, bf16[896,1024]{1,0:T(8,128)(2,1)S(1)}, u32[]{:S(2)}) copy-start(bf16[896,1024]{1,0:T(8,128)(2,1)S(1)} %gather_fusion) | copy-start | bytes 5505028
  100.7 34.7 %copy-start.13 = (bf16[896,1024]{1,0:T(8,128)(2,1)S(1)}, bf16[896,1024]{1,0:T(8,128)(2,1)}, u32[]{:S(2)}) copy-start(bf16[896,1024]{1,0:T(8,128)(2,1)} %add_convert_fusion) | copy-start | bytes 5505028
  135.3 3.6 %copy-start.11 = (bf16[1024,1000]{1,0:T(8,128)(2,1)S(1)}, bf16[1024,1000]{1,0:T(8,128)(2,1)}, u32[]{:S(2)}) copy-start(bf16[1024,1000]{1,0:T(8,128)(2,1)} %all-gather.8.cloned.1.call-done) | copy-start | bytes 6144004
  138.9 3.4 %copy-start.12 = (f32[896,1024]{1,0:T(8,128)S(1)}, f32[896,1024]{1,0:T(8,128)}, u32[]{:S(2)}) copy-start(f32[896,1024]{1,0:T(8,128)} %fusion.23) | copy-start | bytes 11010052
  141.1 1.2 copy-start.14
  169.3 0.9 copy-start.2
  169.3 6.9 %copy-start.1 = (f32[1,64,1024]{2,1,0:T(8,128)S(1)}, f32[1,64,1024]{2,1,0:T(8,128)}, u32[]{:S(2)}) copy-start(f32[1,64,1024]{2,1,0:T(8,128)} %param.11) | copy-start | bytes 786436
  169.3 12.6 %copy-start = (f32[1,64,1000]{2,1,0:T(8,128)S(1)}, f32[1,64,1000]{2,1,0:T(8,128)}, u32[]{:S(2)}) copy-start(f32[1,64,1000]{2,1,0:T(8,128)} %param.12) | copy-start | bytes 768004
  169.3 85.2 %copy-start.6 = (f32[2,64,1024]{2,1,0:T(8,128)S(1)}, f32[2,64,1024]{2,1,0:T(8,128)}, u32[]{:S(2)}) copy-start(f32[2,64,1024]{2,1,0:T(8,128)} %param.14) | copy-start | bytes 1572868
  170.2 88.0 %copy-start.5 = (f32[2,64,1000]{2,1,0:T(8,128)S(1)}, f32[2,64,1000]{2,1,0:T(8,128)}, u32[]{:S(2)}) copy-start(f32[2,64,1000]{2,1,0:T(8,128)} %param.15) | copy-start | bytes 1536004
  170.3 17.2 %collective-permute-start = (bf16[64,1024]{1,0:T(8,128)(2,1)S(1)}, bf16[64,1024]{1,0:T(8,128)(2,1)S(1)}, u32[]{:S(2)}, u32[]{:S(2)}) collective-permute-start(bf16[64,1024]{1,0:T(8,128)(2,1)S(1)} %bitcast_convert_fusion.2), channel_id=1, source_target_pairs={{0,16},{16,32},{32,48},{48,64},{64,80},{80,96},{96,112},{112,128},... | collective-permute-start | bytes 393224 | tf_op jit(solution)/shard_map/ppermute | solution.py:39
  174.3 15.1 %collective-permute-start.3 = (bf16[64,1024]{1,0:T(8,128)(2,1)S(1)}, bf16[64,1024]{1,0:T(8,128)(2,1)S(1)}, u32[]{:S(2)}, u32[]{:S(2)}) collective-permute-start(bf16[64,1024]{1,0:T(8,128)(2,1)S(1)} %bitcast_convert_fusion.2), channel_id=1, source_target_pairs={{16,0},{32,16},{48,32},{64,48},{80,64},{96,80},{112,96},{128,112},... | collective-permute-start | bytes 393224 | tf_op jit(solution)/shard_map/ppermute | solution.py:39
  176.3 13.2 %collective-permute-start.1 = (bf16[64,1024]{1,0:T(8,128)(2,1)S(1)}, bf16[64,1024]{1,0:T(8,128)(2,1)S(1)}, u32[]{:S(2)}, u32[]{:S(2)}) collective-permute-start(bf16[64,1024]{1,0:T(8,128)(2,1)S(1)} %bitcast_convert_fusion.1), channel_id=1, source_target_pairs={{0,16},{16,32},{32,48},{48,64},{64,80},{80,96},{96,112},{112,128},... | collective-permute-start | bytes 393224 | tf_op jit(solution)/shard_map/ppermute | solution.py:39
  179.9 9.5 %collective-permute-start.4 = (bf16[64,1024]{1,0:T(8,128)(2,1)S(1)}, bf16[64,1024]{1,0:T(8,128)(2,1)S(1)}, u32[]{:S(2)}, u32[]{:S(2)}) collective-permute-start(bf16[64,1024]{1,0:T(8,128)(2,1)S(1)} %bitcast_convert_fusion.1), channel_id=1, source_target_pairs={{16,0},{32,16},{48,32},{64,48},{80,64},{96,80},{112,96},{128,112},... | collective-permute-start | bytes 393224 | tf_op jit(solution)/shard_map/ppermute | solution.py:39
  182.5 75.6 %collective-permute-start.2 = (bf16[64,1000]{1,0:T(8,128)(2,1)}, bf16[64,1000]{1,0:T(8,128)(2,1)}, u32[]{:S(2)}, u32[]{:S(2)}) collective-permute-start(bf16[64,1000]{1,0:T(8,128)(2,1)} %bitcast_convert_fusion), channel_id=1, source_target_pairs={{0,16},{16,32},{32,48},{48,64},{64,80},{80,96},{96,112},{112,128},... | collective-permute-start | bytes 384008 | tf_op jit(solution)/shard_map/ppermute | solution.py:39
  187.5 70.7 %collective-permute-start.5 = (bf16[64,1000]{1,0:T(8,128)(2,1)}, bf16[64,1000]{1,0:T(8,128)(2,1)}, u32[]{:S(2)}, u32[]{:S(2)}) collective-permute-start(bf16[64,1000]{1,0:T(8,128)(2,1)} %bitcast_convert_fusion), channel_id=1, source_target_pairs={{16,0},{32,16},{48,32},{64,48},{80,64},{96,80},{112,96},{128,112},... | collective-permute-start | bytes 384008 | tf_op jit(solution)/shard_map/ppermute | solution.py:39
  254.5 61.3 %copy-start.4 = (bf16[64,3048]{1,0:T(8,128)(2,1)S(1)}, bf16[64,3048]{1,0:T(8,128)(2,1)}, u32[]{:S(2)}) copy-start(bf16[64,3048]{1,0:T(8,128)(2,1)} %reduce-scatter.4.cloned.1.call-done) | copy-start | bytes 1170436
  290.4 20.3 %all-to-all-start = ((f32[16,1,2]{2,1,0:T(1,128)}), f32[16,1,2]{2,1,0:T(1,128)S(1)}, u32[]{:S(2)}, u32[]{:S(2)}) async-start(f32[16,1,2]{2,1,0:T(1,128)} %broadcast_in_dim.29), calls=%async_computation | async-start | bytes 16384 | tf_op jit(solution)/shard_map/all_to_all | solution.py:56
  (2 other events, 1.3 us)
Sparse Core Ops, SparseCore 0:
  21.1 38.1 all-gather.3
  61.1 33.3 all-gather.5
  96.3 33.3 all-gather.7
  169.4 85.0 reduce-scatter.3
where the time goes:
time: 327 us; the launch traced here: 326 us
  waiting for transfers between devices  134 us (41%)
  blocking collectives  50.9 us (16%)
  between operations  37 us (11%)
  matrix products  35.6 us (11%)
  starting transfers between devices  30.6 us (9%)
  local copies, waits for them, and re-layouts  21.3 us (7%)
  other arithmetic  16.6 us (5%)
    all_gather x3, waiting for transfers between devices, gather_axes(): nearer = lax.all_gather(value, axes[-1], axis=dim, tiled=True)  65 us
    reduce_scatter x1, waiting for transfers between devices, in_one_piece(): lax.psum_scatter(both, axis, scatter_dimension=dim, tiled=True)  63.8 us
    all_gather x3, blocking collectives, gather_axes(): nearer = lax.all_gather(value, axes[-1], axis=dim, tiled=True)  34.9 us
    ppermute x6, starting transfers between devices, passed_along(): return lax.ppermute(block, axis, route)  17.1 us
    dot_general x3, matrix products, dot_tn(): lax.dot_general(left, right, (((0,), (0,)), ((), ())), preferred_element_...  16.2 us
    psum x2, blocking collectives, over_axes(): value = lax.psum(value, axis)  16 us
    all_to_all x1, starting transfers between devices, copy_for_each(): lax.all_to_all(jnp.broadcast_to(value[None], (peers, *value.shape)), axis...  13.3 us
    unnamed x31, local copies, waits for them, and re-layouts  12.3 us
  transfers between devices with their start and end apart: 11, of which 5 were waited for; matrix products, arithmetic and copies ran while one was open for 7% of the time, Pallas kernels for 0%

commit v1 on v0

--- a/solution.py
+++ b/solution.py
@@ -41,7 +41,7 @@
 
 def over_axes(value, axes):
     for axis in axes:
-        value = lax.psum(value, axis)
+        value = jnp.sum(lax.all_gather(value, axis), axis=0)
     return value
 
 

time: 327 us -> 347 us (1.061)
  local copies, waits for them, and re-layouts: 21.3 us -> 37.2 us
  other arithmetic: 16.6 us -> 25 us
  waiting for transfers between devices: 134 us -> 130 us
    psum x2 -> x0, blocking collectives: 16 us -> none  [over_axes(): value = lax.psum(value, axis)]
    unnamed x31 -> x65, local copies, waits for them, and re-layouts: 12.3 us -> 28.2 us
    unnamed x0 -> x2, blocking collectives: none -> 14.6 us
    reduce_sum x0 -> x14, other arithmetic: none -> 8.43 us  [over_axes(): value = jnp.sum(lax.all_gather(value, axis), axis=0)]
  transfers between devices with their start and end apart: 11 -> 11, of which waited for: 5 -> 5; matrix products, arithmetic and copies ran while one was open for 7% -> 8% of each run, Pallas kernels for 0% -> 0%
where the time goes in v1:
time: 347 us; the launch traced here: 345 us
  waiting for transfers between devices  130 us (37%)
  blocking collectives  49.5 us (14%)
  local copies, waits for them, and re-layouts  37.2 us (11%)
  between operations  37.2 us (11%)
  matrix products  35.6 us (10%)
  starting transfers between devices  30.7 us (9%)
  other arithmetic  25 us (7%)
    all_gather x3, waiting for transfers between devices, gather_axes(): nearer = lax.all_gather(value, axes[-1], axis=dim, tiled=True)  65 us
    reduce_scatter x1, waiting for transfers between devices, in_one_piece(): lax.psum_scatter(both, axis, scatter_dimension=dim, tiled=True)  62 us
    all_gather x3, blocking collectives, gather_axes(): nearer = lax.all_gather(value, axes[-1], axis=dim, tiled=True)  34.9 us
    unnamed x65, local copies, waits for them, and re-layouts  28.2 us
    ppermute x6, starting transfers between devices, passed_along(): return lax.ppermute(block, axis, route)  17.1 us
    dot_general x3, matrix products, dot_tn(): lax.dot_general(left, right, (((0,), (0,)), ((), ())), preferred_element_...  16.2 us
    unnamed x2, blocking collectives  14.6 us
    all_to_all x1, starting transfers between devices, copy_for_each(): lax.all_to_all(jnp.broadcast_to(value[None], (peers, *value.shape)), axis...  13.5 us
  transfers between devices with their start and end apart: 11, of which 5 were waited for; matrix products, arithmetic and copies ran while one was open for 8% of the time, Pallas kernels for 0%

profile of v1, /device:TPU:1, one launch (start us, length us, event | category | flops | bytes accessed | tf_op | source)
XLA Modules:
  0.0 345.4 jit_solution(17089542607751400763)
XLA Ops:
  8.2 12.8 %all_gather.110 = bf16[256,1024]{1,0:T(8,128)(2,1)} all-gather(bf16[64,1024]{1,0:T(8,128)(2,1)S(1)} %fusion.10), channel_id=1, replica_groups=mesh['chain'=16,'dp_0'=4,'dp_1'=4] {'dp_1'}, dimensions={0}, use_global_device_ids=true | all-gather | bytes 655360 | tf_op jit(solution)/shard_map/all_gather | solution.py:23
  22.0 10.7 %all_gather.112 = bf16[256,1024]{1,0:T(8,128)(2,1)} all-gather(bf16[64,1024]{1,0:T(8,128)(2,1)S(1)} %fusion.7), channel_id=1, replica_groups=mesh['chain'=16,'dp_0'=4,'dp_1'=4] {'dp_1'}, dimensions={0}, use_global_device_ids=true | all-gather | bytes 655360 | tf_op jit(solution)/shard_map/all_gather | solution.py:23
  33.8 11.5 %all_gather.114 = bf16[256,1000]{1,0:T(8,128)(2,1)} all-gather(bf16[64,1000]{1,0:T(8,128)(2,1)S(1)} %fusion.4), channel_id=1, replica_groups=mesh['chain'=16,'dp_0'=4,'dp_1'=4] {'dp_1'}, dimensions={0}, use_global_device_ids=true | all-gather | bytes 640000 | tf_op jit(solution)/shard_map/all_gather | solution.py:23
  45.4 7.7 %gather_fusion = bf16[896,1024]{1,0:T(8,128)(2,1)S(1)} fusion(bf16[1792,1024]{1,0:T(8,128)(2,1)} %param.16, s32[1024]{0:T(1024)S(1)} %pad_clamp_fusion), kind=kCustom, calls=%fused_computation | custom fusion | bytes 3673600 | tf_op jit(solution)/shard_map/gather | solution.py:113
  53.1 6.2 %all-gather.4.cloned.1.call-done = bf16[1024,1024]{1,0:T(8,128)(2,1)} async-done(((bf16[256,1024]{1,0:T(8,128)(2,1)}), bf16[1024,1024]{1,0:T(8,128)(2,1)}) %all-gather.4.cloned.1.call-update) | async-done | bytes 2097168 | tf_op jit(solution)/shard_map/all_gather | solution.py:23
  59.3 5.4 %fusion.23 = f32[896,1024]{1,0:T(8,128)} fusion(bf16[896,1024]{1,0:T(8,128)(2,1)S(1)} %gather_fusion, bf16[1024,1024]{1,0:T(8,128)(2,1)} %all-gather.4.cloned.1.call-done), kind=kOutput, calls=%fused_computation.72 | convolution fusion | flops 1879048192 | bytes 7602176 | tf_op jit(solution)/shard_map/dot_general | solution.py:115
  64.7 29.8 %all-gather.6.cloned.1.call-done = bf16[1024,1024]{1,0:T(8,128)(2,1)} async-done(((bf16[256,1024]{1,0:T(8,128)(2,1)}), bf16[1024,1024]{1,0:T(8,128)(2,1)}) %all-gather.6.cloned.1.call-update) | async-done | bytes 2097168 | tf_op jit(solution)/shard_map/all_gather | solution.py:23
  94.5 6.2 %add_convert_fusion = bf16[896,1024]{1,0:T(8,128)(2,1)} fusion(bf16[896,1024]{1,0:T(8,128)(2,1)S(1)} %gather_fusion, bf16[1024,1024]{1,0:T(8,128)(2,1)} %all-gather.6.cloned.1.call-done, f32[896,1024]{1,0:T(8,128)} %fusion.23), kind=kOutput, calls=%fused_computation.3 | convolution fusion | flops 1886388224 | bytes 9437184 | tf_op jit(solution)/shard_map/dot_general | solution.py:118
  100.7 29.1 %all-gather.8.cloned.1.call-done = bf16[1024,1000]{1,0:T(8,128)(2,1)} async-done(((bf16[256,1000]{1,0:T(8,128)(2,1)}), bf16[1024,1000]{1,0:T(8,128)(2,1)}) %all-gather.8.cloned.1.call-update) | async-done | bytes 2048016 | tf_op jit(solution)/shard_map/all_gather | solution.py:23
  129.7 5.6 %multiply_reduce_fusion = (f32[]{:T(128)}, f32[896,1000]{0,1:T(8,128)S(1)}) fusion(s32[896]{0:T(1024)S(1)} %reduce.16, bf16[896,1024]{1,0:T(8,128)(2,1)} %add_convert_fusion, bf16[1024,1000]{1,0:T(8,128)(2,1)} %all-gather.8.cloned.1.call-done), kind=kOutput, calls=%fused_computation.6 | convolution fusion | flops 1839488000 | bytes 7470596 | tf_op jit(solution)/shard_map/dot_general | solution.py:120
  135.3 3.6 %convolution_convert_fusion.2 = bf16[1024,1000]{0,1:T(8,128)(2,1)} fusion(bf16[896,1024]{1,0:T(8,128)(2,1)S(1)} %copy-done.15, f32[896,1000]{0,1:T(8,128)S(1)} %get-tuple-element.59, s32[896]{0:T(1024)S(1)} %reduce.16), kind=kOutput, calls=%fused_computation.12 | convolution fusion | flops 1840512000 | bytes 7470592 | tf_op jit(solution)/shard_map/dot_general | solution.py:77
  142.4 2.7 convolution_convert_fusion
  145.1 9.9 %convolution_convert_fusion.1 = bf16[1024,1024]{0,1:T(8,128)(2,1)} fusion(bf16[896,1024]{1,0:T(8,128)(2,1)} %copy-done.3, f32[896,1024]{1,0:T(8,128)} %fusion.23, bf16[896,1024]{1,0:T(8,128)(2,1)} %copy-done.16, bf16[1024,1024]{1,0:T(8,128)(2,1)} %all-gather.6.cloned.1.call-done), kind=kOutput, calls=%fused_computation.11 | convolution fusion | flops 3767402496 | bytes 11534336 | tf_op jit(solution)/shard_map/dot_general | solution.py:77
  155.0 5.5 %pad_maximum_fusion = bf16[1024,3048]{0,1:T(8,128)(2,1)} fusion(bf16[1024,1000]{0,1:T(8,128)(2,1)} %convolution_convert_fusion.2, bf16[1024,1024]{0,1:T(8,128)(2,1)S(1)} %convolution_convert_fusion, bf16[1024,1024]{0,1:T(8,128)(2,1)} %convolution_convert_fusion.1), kind=kLoop, calls=%fused_computation.1 | loop fusion | flops 18726912 | bytes 12484608 | tf_op jit(solution)/shard_map/concatenate | solution.py:28
  160.5 8.8 %copy.44 = bf16[1024,3048]{1,0:T(8,128)(2,1)} copy(bf16[1024,3048]{0,1:T(8,128)(2,1)} %pad_maximum_fusion) | data formatting | bytes 12484608
  170.3 4.0 %collective-permute-start = (bf16[64,1024]{1,0:T(8,128)(2,1)S(1)}, bf16[64,1024]{1,0:T(8,128)(2,1)S(1)}, u32[]{:S(2)}, u32[]{:S(2)}) collective-permute-start(bf16[64,1024]{1,0:T(8,128)(2,1)S(1)} %bitcast_convert_fusion.2), channel_id=1, source_target_pairs={{0,16},{16,32},{32,48},{48,64},{64,80},{80,96},{96,112},{112,128},... | collective-permute-start | bytes 393224 | tf_op jit(solution)/shard_map/ppermute | solution.py:39
  176.3 3.6 %collective-permute-start.1 = (bf16[64,1024]{1,0:T(8,128)(2,1)S(1)}, bf16[64,1024]{1,0:T(8,128)(2,1)S(1)}, u32[]{:S(2)}, u32[]{:S(2)}) collective-permute-start(bf16[64,1024]{1,0:T(8,128)(2,1)S(1)} %bitcast_convert_fusion.1), channel_id=1, source_target_pairs={{0,16},{16,32},{32,48},{48,64},{64,80},{80,96},{96,112},{112,128},... | collective-permute-start | bytes 393224 | tf_op jit(solution)/shard_map/ppermute | solution.py:39
  182.5 3.6 %collective-permute-start.2 = (bf16[64,1000]{1,0:T(8,128)(2,1)}, bf16[64,1000]{1,0:T(8,128)(2,1)}, u32[]{:S(2)}, u32[]{:S(2)}) collective-permute-start(bf16[64,1000]{1,0:T(8,128)(2,1)} %bitcast_convert_fusion), channel_id=1, source_target_pairs={{0,16},{16,32},{32,48},{48,64},{64,80},{80,96},{96,112},{112,128},... | collective-permute-start | bytes 384008 | tf_op jit(solution)/shard_map/ppermute | solution.py:39
  192.7 62.0 %reduce-scatter.4.cloned.1.call-done = bf16[64,3048]{1,0:T(8,128)(2,1)} async-done(((bf16[1024,3048]{1,0:T(8,128)(2,1)}), bf16[64,3048]{1,0:T(8,128)(2,1)}) %reduce-scatter.4.cloned.1.call-update) | async-done | bytes 390160 | tf_op jit(solution)/shard_map/reduce_scatter | solution.py:29
  254.7 2.4 multiply_reduce_fusion.11
  274.9 8.2 %all-reduce.15 = (f32[4]{0:T(128)S(1)}, f32[4]{0:T(128)S(1)}, f32[4]{0:T(128)S(1)}, f32[4]{0:T(128)S(1)}, f32[4]{0:T(128)S(1)}, /*index=5*/f32[4]{0:T(128)S(1)}, f32[4]{0:T(128)S(1)}) all-reduce(f32[4]{0:T(128)S(1)} %dynamic-update-slice.2, f32[4]{0:T(128)S(1)} %dynamic-update-slice, ...), channel_id=1, replica_groups=mesh['chain'=16,'dp_0'=4,'dp_1'=4] {'dp_0'}, use_global_device_ids=true, to_apply=%add.2 | all-reduce | flops 28 | bytes 224
  296.8 6.4 %all-reduce.14 = (f32[4]{0:T(128)S(1)}, f32[4]{0:T(128)S(1)}, f32[4]{0:T(128)S(1)}, f32[4]{0:T(128)S(1)}, f32[4]{0:T(128)S(1)}, /*index=5*/f32[4]{0:T(128)S(1)}, f32[4]{0:T(128)S(1)}) all-reduce(f32[4]{0:T(128)S(1)} %dynamic-update-slice.3, f32[4]{0:T(128)S(1)} %dynamic-update-slice.1, ...), channel_id=1, replica_groups=mesh['chain'=16,'dp_0'=4,'dp_1'=4] {'dp_1'}, use_global_device_ids=true, to_apply=%add.3 | all-reduce | flops 28 | bytes 224
  309.2 13.5 %all-to-all-start = ((f32[16,1,2]{2,1,0:T(1,128)}), f32[16,1,2]{2,1,0:T(1,128)S(1)}, u32[]{:S(2)}, u32[]{:S(2)}) async-start(f32[16,1,2]{2,1,0:T(1,128)} %broadcast_in_dim.29), calls=%async_computation | async-start | bytes 16384 | tf_op jit(solution)/shard_map/all_to_all | solution.py:56
  326.5 3.2 all-to-all-done
  (114 shorter events, 45.8 us)
Async XLA Ops:
  7.2 38.1 %copy-start.9 = (s32[1,896]{1,0:T(1,128)S(1)}, s32[1,896]{1,0:T(1,128)}, u32[]{:S(2)}) copy-start(s32[1,896]{1,0:T(1,128)} %param.17) | copy-start | bytes 10756
  7.2 52.1 %all-gather.4.cloned.1.call-start = ((), (), s32[]{:S(2)}) async-start(), calls=%async_computation.2 | async-start | bytes 2621440 | tf_op jit(solution)/shard_map/all_gather | solution.py:23
  21.0 73.5 %all-gather.6.cloned.1.call-start = ((), (), s32[]{:S(2)}) async-start(), calls=%async_computation.3 | async-start | bytes 2621440 | tf_op jit(solution)/shard_map/all_gather | solution.py:23
  32.7 97.0 %all-gather.8.cloned.1.call-start = ((), (), s32[]{:S(2)}) async-start(), calls=%async_computation.4 | async-start | bytes 2621440 | tf_op jit(solution)/shard_map/all_gather | solution.py:23
  45.2 209.4 %reduce-scatter.4.cloned.1.call-start = ((), (), s32[]{:S(2)}) async-start(), calls=%async_computation.5 | async-start | bytes 6684672 | tf_op jit(solution)/shard_map/reduce_scatter | solution.py:29
  45.3 7.8 %copy-start.10 = (s32[1,896]{1,0:T(1,128)S(1)}, s32[1,896]{1,0:T(1,128)}, u32[]{:S(2)}) copy-start(s32[1,896]{1,0:T(1,128)} %param.18) | copy-start | bytes 10756
  53.1 41.4 %copy-start.3 = (bf16[896,1024]{1,0:T(8,128)(2,1)}, bf16[896,1024]{1,0:T(8,128)(2,1)S(1)}, u32[]{:S(2)}) copy-start(bf16[896,1024]{1,0:T(8,128)(2,1)S(1)} %gather_fusion) | copy-start | bytes 5505028
  100.7 34.7 %copy-start.15 = (bf16[896,1024]{1,0:T(8,128)(2,1)S(1)}, bf16[896,1024]{1,0:T(8,128)(2,1)}, u32[]{:S(2)}) copy-start(bf16[896,1024]{1,0:T(8,128)(2,1)} %add_convert_fusion) | copy-start | bytes 5505028
  135.3 3.6 %copy-start.11 = (bf16[1024,1000]{1,0:T(8,128)(2,1)S(1)}, bf16[1024,1000]{1,0:T(8,128)(2,1)}, u32[]{:S(2)}) copy-start(bf16[1024,1000]{1,0:T(8,128)(2,1)} %all-gather.8.cloned.1.call-done) | copy-start | bytes 6144004
  138.9 3.4 copy-start.14
  169.3 6.9 %copy-start.1 = (f32[1,64,1024]{2,1,0:T(8,128)S(1)}, f32[1,64,1024]{2,1,0:T(8,128)}, u32[]{:S(2)}) copy-start(f32[1,64,1024]{2,1,0:T(8,128)} %param.11) | copy-start | bytes 786436
  169.3 12.6 %copy-start = (f32[1,64,1000]{2,1,0:T(8,128)S(1)}, f32[1,64,1000]{2,1,0:T(8,128)}, u32[]{:S(2)}) copy-start(f32[1,64,1000]{2,1,0:T(8,128)} %param.12) | copy-start | bytes 768004
  169.3 16.9 %copy-start.13 = (u32[256]{0:T(256)S(1)}, u32[256]{0:T(256)}, u32[]{:S(2)}) copy-start(u32[256]{0:T(256)} %constant.49) | copy-start | bytes 3076
  169.3 17.5 %copy-start.12 = (u32[256]{0:T(256)S(1)}, u32[256]{0:T(256)}, u32[]{:S(2)}) copy-start(u32[256]{0:T(256)} %constant.54) | copy-start | bytes 3076
  169.3 85.4 %copy-start.6 = (f32[2,64,1024]{2,1,0:T(8,128)S(1)}, f32[2,64,1024]{2,1,0:T(8,128)}, u32[]{:S(2)}) copy-start(f32[2,64,1024]{2,1,0:T(8,128)} %param.14) | copy-start | bytes 1572868
  170.2 88.1 %copy-start.5 = (f32[2,64,1000]{2,1,0:T(8,128)S(1)}, f32[2,64,1000]{2,1,0:T(8,128)}, u32[]{:S(2)}) copy-start(f32[2,64,1000]{2,1,0:T(8,128)} %param.15) | copy-start | bytes 1536004
  170.3 19.2 %collective-permute-start = (bf16[64,1024]{1,0:T(8,128)(2,1)S(1)}, bf16[64,1024]{1,0:T(8,128)(2,1)S(1)}, u32[]{:S(2)}, u32[]{:S(2)}) collective-permute-start(bf16[64,1024]{1,0:T(8,128)(2,1)S(1)} %bitcast_convert_fusion.2), channel_id=1, source_target_pairs={{0,16},{16,32},{32,48},{48,64},{64,80},{80,96},{96,112},{112,128},... | collective-permute-start | bytes 393224 | tf_op jit(solution)/shard_map/ppermute | solution.py:39
  174.3 17.1 %collective-permute-start.3 = (bf16[64,1024]{1,0:T(8,128)(2,1)S(1)}, bf16[64,1024]{1,0:T(8,128)(2,1)S(1)}, u32[]{:S(2)}, u32[]{:S(2)}) collective-permute-start(bf16[64,1024]{1,0:T(8,128)(2,1)S(1)} %bitcast_convert_fusion.2), channel_id=1, source_target_pairs={{16,0},{32,16},{48,32},{64,48},{80,64},{96,80},{112,96},{128,112},... | collective-permute-start | bytes 393224 | tf_op jit(solution)/shard_map/ppermute | solution.py:39
  176.3 15.1 %collective-permute-start.1 = (bf16[64,1024]{1,0:T(8,128)(2,1)S(1)}, bf16[64,1024]{1,0:T(8,128)(2,1)S(1)}, u32[]{:S(2)}, u32[]{:S(2)}) collective-permute-start(bf16[64,1024]{1,0:T(8,128)(2,1)S(1)} %bitcast_convert_fusion.1), channel_id=1, source_target_pairs={{0,16},{16,32},{32,48},{48,64},{64,80},{80,96},{96,112},{112,128},... | collective-permute-start | bytes 393224 | tf_op jit(solution)/shard_map/ppermute | solution.py:39
  179.9 11.5 %collective-permute-start.4 = (bf16[64,1024]{1,0:T(8,128)(2,1)S(1)}, bf16[64,1024]{1,0:T(8,128)(2,1)S(1)}, u32[]{:S(2)}, u32[]{:S(2)}) collective-permute-start(bf16[64,1024]{1,0:T(8,128)(2,1)S(1)} %bitcast_convert_fusion.1), channel_id=1, source_target_pairs={{16,0},{32,16},{48,32},{64,48},{80,64},{96,80},{112,96},{128,112},... | collective-permute-start | bytes 393224 | tf_op jit(solution)/shard_map/ppermute | solution.py:39
  182.5 75.8 %collective-permute-start.2 = (bf16[64,1000]{1,0:T(8,128)(2,1)}, bf16[64,1000]{1,0:T(8,128)(2,1)}, u32[]{:S(2)}, u32[]{:S(2)}) collective-permute-start(bf16[64,1000]{1,0:T(8,128)(2,1)} %bitcast_convert_fusion), channel_id=1, source_target_pairs={{0,16},{16,32},{32,48},{48,64},{64,80},{80,96},{96,112},{112,128},... | collective-permute-start | bytes 384008 | tf_op jit(solution)/shard_map/ppermute | solution.py:39
  189.4 68.9 %collective-permute-start.5 = (bf16[64,1000]{1,0:T(8,128)(2,1)}, bf16[64,1000]{1,0:T(8,128)(2,1)}, u32[]{:S(2)}, u32[]{:S(2)}) collective-permute-start(bf16[64,1000]{1,0:T(8,128)(2,1)} %bitcast_convert_fusion), channel_id=1, source_target_pairs={{16,0},{32,16},{48,32},{64,48},{80,64},{96,80},{112,96},{128,112},... | collective-permute-start | bytes 384008 | tf_op jit(solution)/shard_map/ppermute | solution.py:39
  254.7 80.2 %copy-start.4 = (bf16[64,3048]{1,0:T(8,128)(2,1)S(1)}, bf16[64,3048]{1,0:T(8,128)(2,1)}, u32[]{:S(2)}) copy-start(bf16[64,3048]{1,0:T(8,128)(2,1)} %reduce-scatter.4.cloned.1.call-done) | copy-start | bytes 1170436
  309.2 20.5 %all-to-all-start = ((f32[16,1,2]{2,1,0:T(1,128)}), f32[16,1,2]{2,1,0:T(1,128)S(1)}, u32[]{:S(2)}, u32[]{:S(2)}) async-start(f32[16,1,2]{2,1,0:T(1,128)} %broadcast_in_dim.29), calls=%async_computation | async-start | bytes 16384 | tf_op jit(solution)/shard_map/all_to_all | solution.py:56
  (4 other events, 3.5 us)
Sparse Core Ops, SparseCore 0:
  21.1 38.1 all-gather.3
  61.1 33.3 all-gather.5
  96.3 33.3 all-gather.7
  169.5 85.1 reduce-scatter.3
